TPU v7x, 32 devices: a whole 2x2x4 slice. The times are simulated.
32 devices in a mesh: row: 8 (over z, x), col: 2 (over y), depth: 2 (over core).
Axes of the slice: x: 2, y: 2, z: 4, core: 2. Of those that a mesh axis runs over, the one named last changes fastest.
Arguments:
- tokens: bfloat16 [1024, 5376], P('row', 'depth'), may hold values from -6 to 6
- gate_weight: bfloat16 [9216, 5376], P(('col', 'row'), 'depth'), may hold values from -0.078125 to 0.078125
- up_weight: bfloat16 [9216, 5376], P(('col', 'row'), 'depth'), may hold values from -0.078125 to 0.078125
- down_weight: bfloat16 [9216, 5376], P(('col', 'depth'), 'row'), may hold values from -0.09375 to 0.09375
Outputs:
- output: bfloat16 [1024, 5376], P('row', ('col', 'depth'))
All inputs are finite; a program needn't handle non-finite values.
Results may differ from a plain program's by a relative error of at most 0.0049.
Values may be sent and summed in bfloat16 or wider, within the bound.
A program may use at most 128 MiB of HBM per device.

v0:
```python
import jax
import jax.numpy as jnp
from jax import lax
from jax.sharding import PartitionSpec as P


def local(tokens, gate_weight, up_weight, down_weight):
    paired = jnp.stack([gate_weight, up_weight])
    every_token = jnp.einsum(
        "td,gfd->gtf",
        lax.all_gather(tokens, "row", axis=0, tiled=True),
        paired,
        preferred_element_type=jnp.float32,
    )
    partial_sums = lax.all_to_all(every_token, "row", split_axis=1, concat_axis=2, tiled=True)
    share_width = partial_sums.shape[2] // lax.axis_size("depth")
    summed = lax.psum(partial_sums, "depth")
    shares = lax.dynamic_slice_in_dim(summed, lax.axis_index("depth") * share_width, share_width, 2)
    hidden = (jax.nn.silu(shares[0]) * shares[1]).astype(jnp.bfloat16)
    down_terms = jnp.dot(
        hidden,
        lax.all_gather(down_weight, "row", axis=1, tiled=True),
        preferred_element_type=jnp.float32,
    )
    return lax.psum_scatter(down_terms, ("col", "depth"), scatter_dimension=1, tiled=True).astype(
        jnp.bfloat16
    )


def solution(mesh):
    in_specs = (
        P("row", "depth"),
        P(("col", "row"), "depth"),
        P(("col", "row"), "depth"),
        P(("col", "depth"), "row"),
    )
    out_specs = P("row", ("col", "depth"))
    return jax.shard_map(local, mesh=mesh, in_specs=in_specs, out_specs=out_specs, check_vma=False)
```

profile of v0, /device:TPU:0, one launch (start us, length us, event | category | flops | bytes accessed | tf_op | source)
XLA Modules:
  0.0 810.8 jit_solution(2922904456121408201)
XLA Ops:
  6.5 0.0 all-gather.3.cloned.1.call-start
  6.5 0.7 all-gather.3.cloned.1.call-update
  7.3 0.0 all-reduce.2.cloned.1.call-start
  7.3 94.1 %all-gather.3.cloned.1.call-done = bf16[1024,2688]{1,0:T(8,128)(2,1)} async-done(((bf16[128,2688]{1,0:T(8,128)(2,1)}), bf16[1024,2688]{1,0:T(8,128)(2,1)}) %all-gather.3.cloned.1.call-update) | async-done | bytes 5505040 | tf_op jit(solution)/shard_map/all_gather | solution.py:11
  101.4 12.0 %fusion.5 = f32[2,1024,576]{1,2,0:T(8,128)} fusion(bf16[1024,2688]{1,0:T(8,128)(2,1)} %all-gather.3.cloned.1.call-done, bf16[1,576,2688]{2,1,0:T(8,128)(2,1)} %bitcast.29, bf16[1,576,2688]{2,1,0:T(8,128)(2,1)} %bitcast.30), kind=kOutput, calls=%fused_computation.5 | convolution fusion | flops 6344884224 | bytes 16416768 | tf_op jit(solution)/shard_map/td,gfd->gtf/dot_general | solution.py:9
  113.4 8.8 %copy.7 = f32[2,1024,576]{2,0,1:T(2,128)} copy(f32[2,1024,576]{1,2,0:T(8,128)} %fusion.5) | data formatting | bytes 9437184 | tf_op jit(solution)/shard_map/td,gfd->gtf/transpose | solution.py:9
  122.1 118.9 %all_to_all.18 = f32[2,1024,576]{2,0,1:T(2,128)} all-to-all(f32[2,1024,576]{2,0,1:T(2,128)} %copy.7), channel_id=1, replica_groups=mesh['row'=8,'col'=2,'depth'=2] {'row'}, dimensions={1} | all-to-all | bytes 9437184 | tf_op jit(solution)/shard_map/all_to_all | solution.py:15
  241.1 8.7 %copy.11 = f32[2,8,128,576]{2,3,1,0:T(8,128)} copy(f32[2,8,128,576]{3,0,2,1:T(2,128)} %bitcast.27) | data formatting | bytes 9437184 | tf_op jit(solution)/shard_map/all_to_all | solution.py:15
  249.7 0.0 all-reduce.2.cloned.1.call-update
  249.8 0.0 all-gather.5.cloned.1.call-start
  249.8 0.7 all-gather.5.cloned.1.call-update
  250.5 0.0 reduce-scatter.2.cloned.1.call-start
  250.6 27.2 %all-reduce.2.cloned.1.call-done = f32[2,128,4608]{1,2,0:T(8,128)} async-done(((f32[2,128,4608]{1,2,0:T(8,128)}), f32[2,128,4608]{1,2,0:T(8,128)}) %all-reduce.2.cloned.1.call-update) | async-done | bytes 4718608 | tf_op jit(solution)/shard_map/psum | solution.py:17
  277.8 475.7 %all-gather.5.cloned.1.call-done = bf16[2304,5376]{0,1:T(8,128)(2,1)} async-done(((bf16[2304,672]{0,1:T(8,128)(2,1)}), bf16[2304,5376]{0,1:T(8,128)(2,1)}) %all-gather.5.cloned.1.call-update) | async-done | bytes 24772624 | tf_op jit(solution)/shard_map/all_gather | solution.py:22
  753.5 13.3 %fusion.12 = f32[128,5376]{0,1:T(8,128)} fusion(bf16[2304,5376]{0,1:T(8,128)(2,1)} %all-gather.5.cloned.1.call-done, f32[2,128,4608]{1,2,0:T(8,128)} %all-reduce.2.cloned.1.call-done, s32[]{:T(128)S(6)} %add.13, s32[]{:T(128)S(6)} %select_n.3), kind=kOutput, calls=%fused_computation.10 | convolution fusion | flops 3172663296 | bytes 29884424 | tf_op jit(solution)/shard_map/dot_general | solution.py:20
  766.9 0.0 reduce-scatter.2.cloned.1.call-update
  766.9 35.5 %reduce-scatter.2.cloned.1.call-done = f32[128,1344]{0,1:T(8,128)} async-done(((f32[128,5376]{0,1:T(8,128)}), f32[128,1344]{0,1:T(8,128)}) %reduce-scatter.2.cloned.1.call-update) | async-done | bytes 688144 | tf_op jit(solution)/shard_map/reduce_scatter | solution.py:25
  802.4 1.9 convert_element_type.7
Async XLA Ops:
  6.5 94.9 %all-gather.3.cloned.1.call-start = ((), (), s32[]{:S(2)}) async-start(), calls=%async_computation.2 | async-start | bytes 6193152 | tf_op jit(solution)/shard_map/all_gather | solution.py:11
  7.3 270.5 %all-reduce.2.cloned.1.call-start = ((), (), s32[]{:S(2)}) async-start(), calls=%async_computation.3 | async-start | bytes 9437184 | tf_op jit(solution)/shard_map/psum | solution.py:17
  249.8 503.8 %all-gather.5.cloned.1.call-start = ((), (), s32[]{:S(2)}) async-start(), calls=%async_computation.4 | async-start | bytes 27869184 | tf_op jit(solution)/shard_map/all_gather | solution.py:22
  250.5 551.9 %reduce-scatter.2.cloned.1.call-start = ((), (), s32[]{:S(2)}) async-start(), calls=%async_computation.5 | async-start | bytes 3440640 | tf_op jit(solution)/shard_map/reduce_scatter | solution.py:25
Sparse Core Ops, SparseCore 0:
  9.5 91.8 all-gather.2
  249.9 27.8 all-reduce.1
  279.3 474.1 all-gather.4
  767.0 35.2 reduce-scatter.1
where the time goes:
time: 811 us
  waiting for transfers between devices  634 us (78%)
  blocking collectives  119 us (15%)
  matrix products  25.3 us (3%)
  local copies, waits for them, and re-layouts  17.5 us (2%)
  between operations  13.1 us (2%)
    all_gather x1, waiting for transfers between devices, local(): lax.all_gather(down_weight, 'row', axis=1, tiled=True)  476 us
    all_to_all x1, blocking collectives, local(): lax.all_to_all(every_token, 'row', split_axis=1, concat_axis=2, tiled=True)  119 us
    all_gather x1, waiting for transfers between devices, local(): lax.all_gather(tokens, 'row', axis=0, tiled=True)  94.1 us
    reduce_scatter x1, waiting for transfers between devices, local(): lax.psum_scatter(down_terms, ('col', 'depth'), scatter_dimension=1, tiled...  35.5 us
    psum x1, waiting for transfers between devices, local(): summed = lax.psum(partial_sums, 'depth')  27.2 us
  transfers between devices with their start and end apart: 4, of which 4 were waited for; matrix products, arithmetic and copies ran while one was open for 0% of the time, Pallas kernels for 0%

commit v1 on v0

--- a/solution.py
+++ b/solution.py
@@ -2,6 +2,17 @@
 import jax.numpy as jnp
 from jax import lax
 from jax.sharding import PartitionSpec as P
+
+
+def in_blocks(x, dim, count):
+    before, after = (x.shape[:dim], x.shape[dim + 1 :])
+    return jnp.moveaxis(x.reshape(*before, count, -1, *after), dim, 0)
+
+
+def in_order(blocks, dim):
+    blocks = jnp.moveaxis(blocks, 0, dim)
+    shape = blocks.shape
+    return blocks.reshape(*shape[:dim], shape[dim] * shape[dim + 1], *shape[dim + 2 :])
 
 
 def local(tokens, gate_weight, up_weight, down_weight):
@@ -12,7 +23,15 @@
         paired,
         preferred_element_type=jnp.float32,
     )
-    partial_sums = lax.all_to_all(every_token, "row", split_axis=1, concat_axis=2, tiled=True)
+    devices, index = (lax.axis_size("row"), lax.axis_index("row"))
+    parts = in_blocks(every_token, 1, devices)
+    whole = parts
+    for step in range(1, devices):
+        target, source = ((index + step) % devices, (index - step) % devices)
+        sent = lax.dynamic_index_in_dim(parts, target, 0)
+        other = lax.ppermute(sent, "row", [(i, (i + step) % devices) for i in range(devices)])
+        whole = lax.dynamic_update_slice_in_dim(whole, other, source, axis=0)
+    partial_sums = in_order(whole, 2)
     share_width = partial_sums.shape[2] // lax.axis_size("depth")
     summed = lax.psum(partial_sums, "depth")
     shares = lax.dynamic_slice_in_dim(summed, lax.axis_index("depth") * share_width, share_width, 2)

time: 811 us -> 786 us (0.969)
  blocking collectives: 119 us -> 0 us
  waiting for transfers between devices: 634 us -> 713 us
  starting transfers between devices: 0.12 us -> 16.5 us
    all_to_all x1 -> x0, blocking collectives: 119 us -> none  [local(): lax.all_to_all(every_token, 'row', split_axis=1, concat_axis=2, tiled=True)]
    ppermute x0 -> x7, waiting for transfers between devices: none -> 47.5 us  [local(): lax.ppermute(sent, 'row', [(i, (i + step) % devices) for i in range(devic...]
    psum x1, waiting for transfers between devices: 27.2 us -> 58.4 us  [local(): summed = lax.psum(partial_sums, 'depth')]
    ppermute x0 -> x7, starting transfers between devices: none -> 16.4 us  [local(): lax.ppermute(sent, 'row', [(i, (i + step) % devices) for i in range(devic...]
    all_to_all x1 -> x0, local copies, waits for them, and re-layouts: 8.69 us -> none  [local(): lax.all_to_all(every_token, 'row', split_axis=1, concat_axis=2, tiled=True)]
  transfers between devices with their start and end apart: 4 -> 11, of which waited for: 4 -> 7; matrix products, arithmetic and copies ran while one was open for 0% -> 1% of each run, Pallas kernels for 0% -> 0%
where the time goes in v1:
time: 786 us
  waiting for transfers between devices  713 us (91%)
  matrix products  24 us (3%)
  local copies, waits for them, and re-layouts  18 us (2%)
  starting transfers between devices  16.5 us (2%)
  between operations  13.3 us (2%)
    all_gather x1, waiting for transfers between devices, local(): lax.all_gather(down_weight, 'row', axis=1, tiled=True)  476 us
    all_gather x1, waiting for transfers between devices, local(): lax.all_gather(tokens, 'row', axis=0, tiled=True)  94 us
    psum x1, waiting for transfers between devices, local(): summed = lax.psum(partial_sums, 'depth')  58.4 us
    ppermute x7, waiting for transfers between devices, local(): lax.ppermute(sent, 'row', [(i, (i + step) % devices) for i in range(devic...  47.5 us
    reduce_scatter x1, waiting for transfers between devices, local(): lax.psum_scatter(down_terms, ('col', 'depth'), scatter_dimension=1, tiled...  35.5 us
    ppermute x7, starting transfers between devices, local(): lax.ppermute(sent, 'row', [(i, (i + step) % devices) for i in range(devic...  16.4 us
  transfers between devices with their start and end apart: 11, of which 7 were waited for; matrix products, arithmetic and copies ran while one was open for 1% of the time, Pallas kernels for 0%

profile of v1, /device:TPU:0, one launch (start us, length us, event | category | flops | bytes accessed | tf_op | source)
XLA Modules:
  0.0 786.1 jit_solution(4941203555601219812)
XLA Ops:
  7.4 94.0 %all-gather.3.cloned.1.call-done = bf16[1024,2688]{1,0:T(8,128)(2,1)} async-done(((bf16[128,2688]{1,0:T(8,128)(2,1)}), bf16[1024,2688]{1,0:T(8,128)(2,1)}) %all-gather.3.cloned.1.call-update) | async-done | bytes 5505040 | tf_op jit(solution)/shard_map/all_gather | solution.py:22
  101.4 10.6 %fusion = f32[2,576,1024]{2,1,0:T(8,128)S(1)} fusion(bf16[1,576,2688]{2,1,0:T(8,128)(2,1)} %bitcast.50, bf16[1,576,2688]{2,1,0:T(8,128)(2,1)} %bitcast.51, bf16[1024,2688]{1,0:T(8,128)(2,1)} %all-gather.3.cloned.1.call-done), kind=kOutput, calls=%fused_computation | convolution fusion | flops 6344884224 | bytes 16416768 | tf_op jit(solution)/shard_map/td,gfd->gtf/dot_general | solution.py:20
  112.0 1.2 copy.7
  113.2 1.1 copy-done
  114.3 3.6 constant_dynamic-slice_fusion
  119.0 2.4 collective-permute-start.2
  121.4 2.3 collective-permute-start.3
  124.3 5.0 bitcast_bitcast_fusion
  129.2 8.0 %collective-permute-done = f32[1,2,128,576]{2,3,0,1:T(8,128)} collective-permute-done((f32[1,2,128,576]{2,3,0,1:T(8,128)}, f32[1,2,128,576]{2,3,0,1:T(8,128)}, u32[]{:S(2)}, u32[]{:S(2)}) %collective-permute-start) | collective-permute-done | bytes 589856 | tf_op jit(solution)/shard_map/ppermute | solution.py:32
  137.2 2.0 constant_dynamic-update-slice_fusion.6
  139.2 10.0 %collective-permute-start.6 = (f32[1,2,128,576]{2,3,0,1:T(8,128)S(1)}, f32[1,2,128,576]{2,3,0,1:T(8,128)S(1)}, u32[]{:S(2)}, u32[]{:S(2)}) collective-permute-start(f32[1,2,128,576]{2,3,0,1:T(8,128)S(1)} %bitcast.44), channel_id=1, source_target_pairs={{0,28},{4,0},{8,4},{12,8},{16,12},{20,16},{24,20},{28,24},{1,29},{... | collective-permute-start | bytes 1769480 | tf_op jit(solution)/shard_map/ppermute | solution.py:32
  149.2 0.9 constant_dynamic-update-slice_fusion.5
  150.1 34.9 %collective-permute-done.2 = f32[1,2,128,576]{2,3,0,1:T(8,128)S(1)} collective-permute-done((f32[1,2,128,576]{2,3,0,1:T(8,128)S(1)}, f32[1,2,128,576]{2,3,0,1:T(8,128)S(1)}, u32[]{:S(2)}, u32[]{:S(2)}) %collective-permute-start.2) | collective-permute-done | bytes 589856 | tf_op jit(solution)/shard_map/ppermute | solution.py:32
  185.0 0.9 constant_dynamic-update-slice_fusion.4
  185.8 0.9 constant_dynamic-update-slice_fusion.3
  186.7 0.9 constant_dynamic-update-slice_fusion.2
  187.6 0.9 constant_dynamic-update-slice_fusion.1
  188.5 4.6 collective-permute-done.6
  193.1 0.9 constant_dynamic-update-slice_fusion
  194.7 58.4 %all-reduce.2.cloned.1.call-done = f32[2,128,4608]{1,2,0:T(8,128)} async-done(((f32[2,128,4608]{1,2,0:T(8,128)}), f32[2,128,4608]{1,2,0:T(8,128)}) %all-reduce.2.cloned.1.call-update) | async-done | bytes 4718608 | tf_op jit(solution)/shard_map/psum | solution.py:36
  253.1 475.7 %all-gather.5.cloned.1.call-done = bf16[2304,5376]{0,1:T(8,128)(2,1)} async-done(((bf16[2304,672]{0,1:T(8,128)(2,1)}), bf16[2304,5376]{0,1:T(8,128)(2,1)}) %all-gather.5.cloned.1.call-update) | async-done | bytes 24772624 | tf_op jit(solution)/shard_map/all_gather | solution.py:41
  728.9 13.3 %fusion.7 = f32[128,5376]{0,1:T(8,128)} fusion(bf16[2304,5376]{0,1:T(8,128)(2,1)} %all-gather.5.cloned.1.call-done, f32[2,128,4608]{1,2,0:T(8,128)} %all-reduce.2.cloned.1.call-done, s32[]{:T(128)S(6)} %add.162, s32[]{:T(128)S(6)} %select_n.133), kind=kOutput, calls=%fused_computation.10 | convolution fusion | flops 3172663296 | bytes 29884424 | tf_op jit(solution)/shard_map/dot_general | solution.py:39
  742.2 35.5 %reduce-scatter.2.cloned.1.call-done = f32[128,1344]{0,1:T(8,128)} async-done(((f32[128,5376]{0,1:T(8,128)}), f32[128,1344]{0,1:T(8,128)}) %reduce-scatter.2.cloned.1.call-update) | async-done | bytes 688144 | tf_op jit(solution)/shard_map/reduce_scatter | solution.py:44
  777.7 1.9 convert_element_type.7
  (17 shorter events, 3.2 us)
Async XLA Ops:
  6.5 94.9 %all-gather.3.cloned.1.call-start = ((), (), s32[]{:S(2)}) async-start(), calls=%async_computation.1 | async-start | bytes 6193152 | tf_op jit(solution)/shard_map/all_gather | solution.py:22
  7.3 245.9 %all-reduce.2.cloned.1.call-start = ((), (), s32[]{:S(2)}) async-start(), calls=%async_computation.2 | async-start | bytes 9437184 | tf_op jit(solution)/shard_map/psum | solution.py:36
  112.0 2.3 copy-start
  117.9 19.4 %collective-permute-start = (f32[1,2,128,576]{2,3,0,1:T(8,128)}, f32[1,2,128,576]{2,3,0,1:T(8,128)}, u32[]{:S(2)}, u32[]{:S(2)}) collective-permute-start(f32[1,2,128,576]{2,3,0,1:T(8,128)} %bitcast.5), channel_id=1, source_target_pairs={{0,4},{4,8},{8,12},{12,16},{16,20},{20,24},{24,28},{28,0},{1,5},{5... | collective-permute-start | bytes 1769480 | tf_op jit(solution)/shard_map/ppermute | solution.py:32
  118.4 20.8 %collective-permute-start.1 = (f32[1,2,128,576]{2,3,0,1:T(8,128)S(1)}, f32[1,2,128,576]{2,3,0,1:T(8,128)S(1)}, u32[]{:S(2)}, u32[]{:S(2)}) collective-permute-start(f32[1,2,128,576]{2,3,0,1:T(8,128)S(1)} %bitcast.49), channel_id=1, source_target_pairs={{0,8},{4,12},{8,16},{12,20},{16,24},{20,28},{24,0},{28,4},{1,9},{5... | collective-permute-start | bytes 1769480 | tf_op jit(solution)/shard_map/ppermute | solution.py:32
  119.0 66.0 %collective-permute-start.2 = (f32[1,2,128,576]{2,3,0,1:T(8,128)S(1)}, f32[1,2,128,576]{2,3,0,1:T(8,128)S(1)}, u32[]{:S(2)}, u32[]{:S(2)}) collective-permute-start(f32[1,2,128,576]{2,3,0,1:T(8,128)S(1)} %bitcast.48), channel_id=1, source_target_pairs={{0,12},{4,16},{8,20},{12,24},{16,28},{20,0},{24,4},{28,8},{1,13},{... | collective-permute-start | bytes 1769480 | tf_op jit(solution)/shard_map/ppermute | solution.py:32
  121.4 64.5 %collective-permute-start.3 = (f32[1,2,128,576]{2,3,0,1:T(8,128)S(1)}, f32[1,2,128,576]{2,3,0,1:T(8,128)S(1)}, u32[]{:S(2)}, u32[]{:S(2)}) collective-permute-start(f32[1,2,128,576]{2,3,0,1:T(8,128)S(1)} %bitcast.47), channel_id=1, source_target_pairs={{0,16},{4,20},{8,24},{12,28},{16,0},{20,4},{24,8},{28,12},{1,17},{... | collective-permute-start | bytes 1769480 | tf_op jit(solution)/shard_map/ppermute | solution.py:32
  123.7 63.0 %collective-permute-start.4 = (f32[1,2,128,576]{2,3,0,1:T(8,128)S(1)}, f32[1,2,128,576]{2,3,0,1:T(8,128)S(1)}, u32[]{:S(2)}, u32[]{:S(2)}) collective-permute-start(f32[1,2,128,576]{2,3,0,1:T(8,128)S(1)} %bitcast.46), channel_id=1, source_target_pairs={{0,20},{4,24},{8,28},{12,0},{16,4},{20,8},{24,12},{28,16},{1,21},{... | collective-permute-start | bytes 1769480 | tf_op jit(solution)/shard_map/ppermute | solution.py:32
  137.2 50.4 %collective-permute-start.5 = (f32[1,2,128,576]{2,3,0,1:T(8,128)S(1)}, f32[1,2,128,576]{2,3,0,1:T(8,128)S(1)}, u32[]{:S(2)}, u32[]{:S(2)}) collective-permute-start(f32[1,2,128,576]{2,3,0,1:T(8,128)S(1)} %bitcast.45), channel_id=1, source_target_pairs={{0,24},{4,28},{8,0},{12,4},{16,8},{20,12},{24,16},{28,20},{1,25},{... | collective-permute-start | bytes 1769480 | tf_op jit(solution)/shard_map/ppermute | solution.py:32
  139.2 53.9 %collective-permute-start.6 = (f32[1,2,128,576]{2,3,0,1:T(8,128)S(1)}, f32[1,2,128,576]{2,3,0,1:T(8,128)S(1)}, u32[]{:S(2)}, u32[]{:S(2)}) collective-permute-start(f32[1,2,128,576]{2,3,0,1:T(8,128)S(1)} %bitcast.44), channel_id=1, source_target_pairs={{0,28},{4,0},{8,4},{12,8},{16,12},{20,16},{24,20},{28,24},{1,29},{... | collective-permute-start | bytes 1769480 | tf_op jit(solution)/shard_map/ppermute | solution.py:32
  193.9 534.9 %all-gather.5.cloned.1.call-start = ((), (), s32[]{:S(2)}) async-start(), calls=%async_computation.3 | async-start | bytes 27869184 | tf_op jit(solution)/shard_map/all_gather | solution.py:41
  194.7 583.0 %reduce-scatter.2.cloned.1.call-start = ((), (), s32[]{:S(2)}) async-start(), calls=%async_computation.4 | async-start | bytes 3440640 | tf_op jit(solution)/shard_map/reduce_scatter | solution.py:44
Sparse Core Ops, SparseCore 0:
  9.5 91.8 all-gather.2
  194.1 59.0 all-reduce.1
  254.7 474.1 all-gather.4
  742.4 35.2 reduce-scatter.1
